TPU v7x, 32 devices: a whole 2x2x4 slice. The times are simulated.
32 devices in a mesh: samp: 4 (over y, x), snp: 8 (over z, core).
Axes of the slice: x: 2, y: 2, z: 4, core: 2. Of those that a mesh axis runs over, the one named last changes fastest.
Arguments:
- genotypes: int32 [8192, 8192], P('samp', 'snp'), may hold values from 0 to 2
- win_lo: int32 [8192], P('snp'), may hold values from 0 to 8191, as said below
- win_hi: int32 [8192], P('snp'), may hold values from 0 to 8191, as said below
- annotation: int32 [8192], P('snp'), may hold values from 0 to 127
- chromosome: int32 [8192], P('snp'), may hold values from 0 to 21, never falling along the last dimension, each value on 1 to 512 neighbouring positions
- chi_square: float32 [8192], P('snp'), may hold values from 0.3 to 60
Outputs:
- annotation_scores: float32 [128, 8192], P('snp')
- gram: float32 [128, 128], replicated
- moments: float32 [2, 128], replicated
- totals: float32 [2], replicated
Inputs may be any that keep to these rules, and one draw needn't show every extreme that they name: i - 512 <= win_lo[i] <= i, nondecreasing in i; the distance 512 is reached. i <= win_hi[i] <= i + 512, nondecreasing in i; the distance 512 is reached.
All inputs are finite; a program needn't handle non-finite values.
Results may differ from a plain program's by a relative error of at most 0.0003.
The roundings to bfloat16 on the way count: a program that leaves them out, or rounds other values in their place, can miss the bound.
Values may be sent and summed in bfloat16 or wider, within the bound.
A program may use at most 64 MiB of HBM per device.

v0:
```python
import jax
import jax.numpy as jnp
from jax import lax
from jax.sharding import PartitionSpec as P

A = 128


def extended(cells, sides, width):
    for axis, dim in sides:
        count = lax.axis_size(axis)
        ends = count - 1
        head = lax.slice_in_dim(cells, 0, width, axis=dim)
        tail = lax.slice_in_dim(cells, cells.shape[dim] - width, cells.shape[dim], axis=dim)
        cells = jnp.concatenate(
            [
                lax.ppermute(tail, axis, [(i, (i + 1) % count) for i in range(ends)]),
                cells,
                lax.ppermute(head, axis, [((i + 1) % count, i) for i in range(ends)]),
            ],
            axis=dim,
        )
    return cells


def body(genotypes, win_lo, win_hi, annotation, chromosome, chi_square):
    samp_rows, block_cols = genotypes.shape
    reach = block_cols // 2
    samp_count = lax.axis_size("samp")
    total_samples = samp_rows * samp_count
    dosage = genotypes.astype(jnp.float32)
    dose_sums, dose_squares = lax.psum((jnp.sum(dosage, 0), jnp.sum(dosage * dosage, 0)), "samp")
    mean_dose = dose_sums / total_samples
    variance = dose_squares / total_samples - mean_dose * mean_dose
    standard = ((dosage - mean_dose) * lax.rsqrt(variance + 1e-05)).astype(jnp.bfloat16)
    first_snp = lax.axis_index("snp") * block_cols
    labels = jnp.arange(A, dtype=jnp.int32)
    own_labels = jnp.stack([annotation, chromosome]).astype(jnp.bfloat16)
    wide_z, wide_labels = (
        extended(standard, (("snp", 1),), reach),
        extended(own_labels, (("snp", 1),), reach),
    )
    annot_wide = wide_labels[0].astype(jnp.int32)
    chrom_wide = wide_labels[1].astype(jnp.int32)
    span = wide_z.shape[1] - block_cols + reach

    def tile_piece(row_start, count):
        band = row_start // reach * reach
        rows_z = lax.dynamic_slice_in_dim(standard, row_start, count, 1)
        cols_z = lax.dynamic_slice_in_dim(wide_z, band, span, 1)
        return lax.dot_general(
            rows_z, cols_z, (((0,), (0,)), ((), ())), preferred_element_type=jnp.float32
        )

    share = block_cols // samp_count
    row_start = jnp.int32(0)
    tile = lax.psum_scatter(
        jnp.concatenate(
            [
                tile_piece(row_start + offset * share, share)
                for offset in range(share * lax.axis_size("samp") // share)
            ],
            0,
        ),
        "samp",
        scatter_dimension=0,
        tiled=True,
    )
    row_begin = lax.axis_index("samp") * share
    row_start = row_begin + 0
    band = row_start // reach * reach
    corr = tile / total_samples
    square = corr * corr
    adjusted = square - (1.0 - square) / (total_samples - 2)
    col_ids = first_snp + band - reach + jnp.arange(span, dtype=jnp.int32)
    lower_end = lax.dynamic_slice_in_dim(win_lo, row_start, share)
    upper_end = lax.dynamic_slice_in_dim(win_hi, row_start, share)
    chrom_rows = lax.dynamic_slice_in_dim(chromosome, row_start, share)
    chrom_cols = lax.dynamic_slice_in_dim(chrom_wide, band, span)
    annot_cols = lax.dynamic_slice_in_dim(annot_wide, band, span)
    inside = (col_ids[None, :] >= lower_end[:, None]) & (col_ids[None, :] <= upper_end[:, None])
    inside = inside & (chrom_cols[None, :] == chrom_rows[:, None])
    kept = jnp.where(inside, adjusted, 0.0)
    member = (annot_cols[:, None] == labels[None, :]).astype(jnp.float32)
    part_scores = lax.dot_general(
        member,
        kept,
        (((0,), (1,)), ((), ())),
        precision=lax.Precision.HIGHEST,
        preferred_element_type=jnp.float32,
    )
    scores = lax.all_gather(part_scores, "samp", axis=1, tiled=True)
    weights = 1.0 / jnp.sum(scores, 0)
    weighted = scores * weights[None, :]
    gram_part = lax.dot_general(
        weighted,
        scores,
        (((1,), (1,)), ((), ())),
        precision=lax.Precision.HIGHEST,
        preferred_element_type=jnp.float32,
    )
    moment_part = jnp.stack([jnp.sum(weighted, 1), jnp.sum(weighted * chi_square[None, :], 1)])
    total_part = jnp.stack([jnp.sum(weights), jnp.sum(weights * chi_square)])
    gram, moments, totals = lax.psum((gram_part, moment_part, total_part), "snp")
    snp_total = block_cols * lax.axis_size("snp")
    scale = A / snp_total
    regrouped = lax.all_to_all(scores, "snp", split_axis=0, concat_axis=1, tiled=True)
    return (regrouped, scale * gram, scale * moments, totals / snp_total)


def solution(mesh):
    in_specs = (P("samp", "snp"), P("snp"), P("snp"), P("snp"), P("snp"), P("snp"))
    out_specs = (P("snp", None), P(), P(), P())
    return jax.shard_map(body, mesh=mesh, in_specs=in_specs, out_specs=out_specs, check_vma=False)
```

profile of v0, /device:TPU:0, one launch (start us, length us, event | category | flops | bytes accessed | tf_op | source)
XLA Modules:
  0.0 220.2 jit_solution(12471998760176331040)
XLA Ops:
  7.2 4.5 %convert_reduce_fusion = (f32[1024]{0:T(1024)S(1)}, f32[1024]{0:T(1024)S(1)}) fusion(s32[2048,1024]{1,0:T(8,128)} %param.6), kind=kLoop, calls=%fused_computation.2 | loop fusion | flops 8386560 | bytes 8396800 | tf_op jit(solution)/shard_map/reduce_sum | solution.py:32
  11.7 11.5 %all-reduce.1 = (f32[1024]{0:T(1024)S(1)}, f32[1024]{0:T(1024)S(1)}) all-reduce(f32[1024]{0:T(1024)S(1)} %get-tuple-element.5, f32[1024]{0:T(1024)S(1)} %get-tuple-element.4), channel_id=1, replica_groups=mesh['samp'=4,'snp'=8] {'samp'}, use_global_device_ids=true, to_apply=%region_3.0 | all-reduce | flops 2048 | bytes 16384 | tf_op jit(solution)/shard_map/psum | solution.py:32
  23.3 4.7 %multiply_convert_fusion = bf16[2048,1024]{1,0:T(8,128)(2,1)S(1)} fusion(s32[2048,1024]{1,0:T(8,128)} %param.6, f32[1024]{0:T(1024)S(1)} %get-tuple-element.22, f32[1024]{0:T(1024)S(1)} %get-tuple-element.21), kind=kLoop, calls=%fused_computation | loop fusion | flops 8388608 | bytes 12591104 | tf_op jit(solution)/shard_map/convert_element_type | solution.py:35
  28.3 1.4 collective-permute-start.2
  29.8 1.3 collective-permute-start.3
  31.1 2.3 %collective-permute-done.2 = bf16[2048,512]{1,0:T(8,128)(2,1)S(1)} collective-permute-done((bf16[2048,512]{1,0:T(8,128)(2,1)S(1)}, bf16[2048,512]{1,0:T(8,128)(2,1)S(1)}, u32[]{:S(2)}, u32[]{:S(2)}) %collective-permute-start.2) | collective-permute-done | bytes 2097184 | tf_op jit(solution)/shard_map/ppermute | solution.py:17
  33.4 1.8 fusion.2
  35.2 1.8 fusion.3
  37.5 1.8 fusion.1
  39.3 1.8 fusion
  41.1 2.9 %pad_maximum_fusion.2 = f32[1024,1536]{1,0:T(8,128)} fusion(f32[256,1536]{1,0:T(8,128)S(1)} %fusion, f32[256,1536]{1,0:T(8,128)S(1)} %fusion.1, f32[256,1536]{1,0:T(8,128)S(1)} %fusion.2, f32[256,1536]{1,0:T(8,128)S(1)} %fusion.3), kind=kLoop, calls=%fused_computation.5 | loop fusion | flops 4718592 | bytes 12582912 | tf_op jit(solution)/shard_map/concatenate | solution.py:58
  44.8 23.7 %collective-permute-start = (bf16[2,512]{1,0:T(2,128)(2,1)S(1)}, bf16[2,512]{1,0:T(2,128)(2,1)S(1)}, u32[]{:S(2)}, u32[]{:S(2)}) collective-permute-start(bf16[2,512]{1,0:T(2,128)(2,1)S(1)} %get-tuple-element.18), channel_id=1, source_target_pairs={{0,1},{1,2},{2,3},{3,4},{4,5},{5,6},{6,7},{8,9},{9,10},{10,11},{11... | collective-permute-start | bytes 6152 | tf_op jit(solution)/shard_map/ppermute | solution.py:17
  68.5 1.3 collective-permute-start.1
  71.4 1.4 collective-permute-done.1
  72.9 62.5 %reduce-scatter.2.cloned.1.call-done = f32[256,1536]{1,0:T(8,128)} async-done(((f32[1024,1536]{1,0:T(8,128)}), f32[256,1536]{1,0:T(8,128)}) %reduce-scatter.2.cloned.1.call-update) | async-done | bytes 1572880 | tf_op jit(solution)/shard_map/reduce_scatter | solution.py:57
  135.5 3.0 %fusion.4 = f32[128,256]{1,0:T(8,128)S(1)} fusion(f32[256,1536]{1,0:T(8,128)} %reduce-scatter.2.cloned.1.call-done, s32[1536]{0:T(1024)S(1)} %get-tuple-element.23, s32[1536]{0:T(1024)S(1)} %iota_add_fusion, s32[256]{0:T(256)S(1)} %dynamic_slice.41, s32[256]{0:T(256)S(1)} %dynamic_slice.38, s32[256]{0:T(256)S(1)} %dynamic_slice.37, ...), kind=kOutput, calls=%fused_computation.10 | convolution fusion | flops 608698368 | bytes 1725440 | tf_op jit(solution)/shard_map/dot_general | solution.py:85
  138.5 10.6 %all_gather.3 = f32[128,1024]{1,0:T(8,128)} all-gather(f32[128,256]{1,0:T(8,128)S(1)} %fusion.4), channel_id=1, replica_groups=mesh['samp'=4,'snp'=8] {'samp'}, dimensions={1}, use_global_device_ids=true | all-gather | bytes 655360 | tf_op jit(solution)/shard_map/all_gather | solution.py:92
  150.8 2.4 %fusion.30 = f32[128,128]{1,0:T(8,128)} fusion(f32[128,1024]{1,0:T(8,128)} %all_gather.3, f32[1024]{0:T(1024)S(1)} %get-tuple-element.20), kind=kOutput, calls=%fused_computation.39 | convolution fusion | flops 201457664 | bytes 593920 | tf_op jit(solution)/shard_map/dot_general | solution.py:95
  153.3 4.6 %all-to-all-start = ((f32[8,16,1024]{2,1,0:T(8,128)}), f32[8,16,1024]{2,1,0:T(8,128)S(1)}, u32[]{:S(2)}, u32[]{:S(2)}) async-start(f32[8,16,1024]{2,1,0:T(8,128)} %bitcast), calls=%async_computation.1 | async-start | bytes 1048576 | tf_op jit(solution)/shard_map/all_to_all | solution.py:107
  157.9 1.4 pad_maximum_fusion.10
  159.3 1.2 multiply_reduce_fusion.1
  160.5 18.6 %all-reduce = (f32[2,128]{1,0:T(2,128)S(1)}, f32[2]{0:T(128)S(1)}) all-reduce(f32[2,128]{1,0:T(2,128)S(1)} %pad_maximum_fusion.9, f32[2]{0:T(128)S(1)} %pad_maximum_fusion.10), channel_id=1, replica_groups=mesh['samp'=4,'snp'=8] {'snp'}, use_global_device_ids=true, to_apply=%region_9.10 | all-reduce | flops 258 | bytes 2064 | tf_op jit(solution)/shard_map/psum | solution.py:104
  180.1 30.9 %all-reduce.4.cloned.1.call-done = f32[128,128]{1,0:T(8,128)} async-done(((f32[128,128]{1,0:T(8,128)}), f32[128,128]{1,0:T(8,128)}) %all-reduce.4.cloned.1.call-update) | async-done | bytes 65552 | tf_op jit(solution)/shard_map/psum | solution.py:104
  211.1 1.5 broadcast_multiply_fusion
  (33 shorter events, 6.8 us)
Async XLA Ops:
  7.2 128.3 %reduce-scatter.2.cloned.1.call-start = ((), (), s32[]{:S(2)}) async-start(), calls=%async_computation.2 | async-start | bytes 7864320 | tf_op jit(solution)/shard_map/reduce_scatter | solution.py:57
  28.3 5.1 %collective-permute-start.2 = (bf16[2048,512]{1,0:T(8,128)(2,1)S(1)}, bf16[2048,512]{1,0:T(8,128)(2,1)S(1)}, u32[]{:S(2)}, u32[]{:S(2)}) collective-permute-start(bf16[2048,512]{1,0:T(8,128)(2,1)S(1)} %get-tuple-element.14), channel_id=1, source_target_pairs={{0,1},{1,2},{2,3},{3,4},{4,5},{5,6},{6,7},{8,9},{9,10},{10,11},{11... | collective-permute-start | bytes 6291464 | tf_op jit(solution)/shard_map/ppermute | solution.py:17
  29.8 7.7 %collective-permute-start.3 = (bf16[2048,512]{1,0:T(8,128)(2,1)S(1)}, bf16[2048,512]{1,0:T(8,128)(2,1)S(1)}, u32[]{:S(2)}, u32[]{:S(2)}) collective-permute-start(bf16[2048,512]{1,0:T(8,128)(2,1)S(1)} %get-tuple-element.15), channel_id=1, source_target_pairs={{1,0},{2,1},{3,2},{4,3},{5,4},{6,5},{7,6},{9,8},{10,9},{11,10},{12... | collective-permute-start | bytes 6291464 | tf_op jit(solution)/shard_map/ppermute | solution.py:19
  44.0 0.7 copy-start.2
  44.0 0.7 copy-start.1
  44.1 106.2 %copy-start = (f32[1024]{0:T(1024)S(1)}, f32[1024]{0:T(1024)}, u32[]{:S(2)}) copy-start(f32[1024]{0:T(1024)} %param.11) | copy-start | bytes 12292
  44.1 167.0 %all-reduce.4.cloned.1.call-start = ((), (), s32[]{:S(2)}) async-start(), calls=%async_computation.3 | async-start | bytes 131072 | tf_op jit(solution)/shard_map/psum | solution.py:104
  44.8 26.6 %collective-permute-start = (bf16[2,512]{1,0:T(2,128)(2,1)S(1)}, bf16[2,512]{1,0:T(2,128)(2,1)S(1)}, u32[]{:S(2)}, u32[]{:S(2)}) collective-permute-start(bf16[2,512]{1,0:T(2,128)(2,1)S(1)} %get-tuple-element.18), channel_id=1, source_target_pairs={{0,1},{1,2},{2,3},{3,4},{4,5},{5,6},{6,7},{8,9},{9,10},{10,11},{11... | collective-permute-start | bytes 6152 | tf_op jit(solution)/shard_map/ppermute | solution.py:17
  68.5 4.3 %collective-permute-start.1 = (bf16[2,512]{1,0:T(2,128)(2,1)S(1)}, bf16[2,512]{1,0:T(2,128)(2,1)S(1)}, u32[]{:S(2)}, u32[]{:S(2)}) collective-permute-start(bf16[2,512]{1,0:T(2,128)(2,1)S(1)} %get-tuple-element.19), channel_id=1, source_target_pairs={{1,0},{2,1},{3,2},{4,3},{5,4},{6,5},{7,6},{9,8},{10,9},{11,10},{12... | collective-permute-start | bytes 6152 | tf_op jit(solution)/shard_map/ppermute | solution.py:19
  153.3 59.3 %all-to-all-start = ((f32[8,16,1024]{2,1,0:T(8,128)}), f32[8,16,1024]{2,1,0:T(8,128)S(1)}, u32[]{:S(2)}, u32[]{:S(2)}) async-start(f32[8,16,1024]{2,1,0:T(8,128)} %bitcast), calls=%async_computation.1 | async-start | bytes 1048576 | tf_op jit(solution)/shard_map/all_to_all | solution.py:107
Sparse Core Ops, SparseCore 0:
  44.2 91.2 reduce-scatter.1
  153.4 57.6 all-reduce.3
where the time goes:
time: 221 us; the launch traced here: 220 us
  waiting for transfers between devices  97.7 us (44%)
  blocking collectives  40.8 us (18%)
  starting transfers between devices  32.4 us (15%)
  other arithmetic  19 us (9%)
  between operations  14.2 us (6%)
  matrix products  12.7 us (6%)
  local copies, waits for them, and re-layouts  3.39 us (2%)
    reduce_scatter x1, waiting for transfers between devices, body(): lax.psum_scatter(jnp.concatenate([tile_piece(row_start + offset * share,...  62.5 us
    psum x1, waiting for transfers between devices, body(): lax.psum((gram_part, moment_part, total_part), 'snp')  30.9 us
    ppermute x2, starting transfers between devices, extended(): lax.ppermute(tail, axis, [(i, (i + 1) % count) for i in range(ends)])  25.1 us
    psum x1, blocking collectives, body(): lax.psum((gram_part, moment_part, total_part), 'snp')  18.6 us
    psum x1, blocking collectives, body(): lax.psum((jnp.sum(dosage, 0), jnp.sum(dosage * dosage, 0)), 'samp')  11.5 us
    all_gather x1, blocking collectives, body(): scores = lax.all_gather(part_scores, 'samp', axis=1, tiled=True)  10.6 us
    dot_general x4, matrix products, tile_piece(): lax.dot_general(rows_z, cols_z, (((0,), (0,)), ((), ())), preferred_eleme...  7.27 us
    convert_element_type x1, other arithmetic, body(): ((dosage - mean_dose) * lax.rsqrt(variance + 1e-05)).astype(jnp.bfloat16)  4.68 us
  transfers between devices with their start and end apart: 7, of which 5 were waited for; matrix products, arithmetic and copies ran while one was open for 5% of the time, Pallas kernels for 0%

commit v1 on v0

--- a/solution.py
+++ b/solution.py
@@ -104,7 +104,16 @@
     gram, moments, totals = lax.psum((gram_part, moment_part, total_part), "snp")
     snp_total = block_cols * lax.axis_size("snp")
     scale = A / snp_total
-    regrouped = lax.all_to_all(scores, "snp", split_axis=0, concat_axis=1, tiled=True)
+    _detail_tasks = lambda local_block, in_dim, at_axis: jnp.concatenate(
+        jax.lax.all_to_all(
+            jnp.stack(jnp.split(local_block, jax.lax.axis_size("snp"), axis=in_dim), axis=0),
+            concat_axis=0,
+            axis_name="snp",
+            split_axis=0,
+        ),
+        at_axis,
+    )
+    regrouped = _detail_tasks(scores, 0, 1)
     return (regrouped, scale * gram, scale * moments, totals / snp_total)
 
 

time: 221 us -> 218 us (0.986)
  waiting for transfers between devices: 97.7 us -> 92.3 us
  local copies, waits for them, and re-layouts: 3.39 us -> 8.47 us
    psum x1, waiting for transfers between devices: 30.9 us -> 25.6 us  [body(): lax.psum((gram_part, moment_part, total_part), 'snp')]
    unnamed x6 -> x13, local copies, waits for them, and re-layouts: 0.61 us -> 5.05 us
  transfers between devices with their start and end apart: 7 -> 7, of which waited for: 5 -> 5; matrix products, arithmetic and copies ran while one was open for 5% -> 6% of each run, Pallas kernels for 0% -> 0%
where the time goes in v1:
time: 218 us; the launch traced here: 217 us
  waiting for transfers between devices  92.3 us (42%)
  blocking collectives  41.3 us (19%)
  starting transfers between devices  32.3 us (15%)
  other arithmetic  16.9 us (8%)
  between operations  14.2 us (7%)
  matrix products  11.5 us (5%)
  local copies, waits for them, and re-layouts  8.47 us (4%)
    reduce_scatter x1, waiting for transfers between devices, body(): lax.psum_scatter(jnp.concatenate([tile_piece(row_start + offset * share,...  62.5 us
    psum x1, waiting for transfers between devices, body(): lax.psum((gram_part, moment_part, total_part), 'snp')  25.6 us
    ppermute x2, starting transfers between devices, extended(): lax.ppermute(tail, axis, [(i, (i + 1) % count) for i in range(ends)])  25.1 us
    psum x1, blocking collectives, body(): lax.psum((gram_part, moment_part, total_part), 'snp')  19.6 us
    psum x1, blocking collectives, body(): lax.psum((jnp.sum(dosage, 0), jnp.sum(dosage * dosage, 0)), 'samp')  11.5 us
    all_gather x1, blocking collectives, body(): scores = lax.all_gather(part_scores, 'samp', axis=1, tiled=True)  10.1 us
    dot_general x4, matrix products, tile_piece(): lax.dot_general(rows_z, cols_z, (((0,), (0,)), ((), ())), preferred_eleme...  7.27 us
    unnamed x13, local copies, waits for them, and re-layouts  5.05 us
  transfers between devices with their start and end apart: 7, of which 5 were waited for; matrix products, arithmetic and copies ran while one was open for 6% of the time, Pallas kernels for 0%

profile of v1, /device:TPU:0, one launch (start us, length us, event | category | flops | bytes accessed | tf_op | source)
XLA Modules:
  0.0 217.1 jit_solution(8970355465411531668)
XLA Ops:
  7.2 4.5 %convert_reduce_fusion = (f32[1024]{0:T(1024)S(1)}, f32[1024]{0:T(1024)S(1)}) fusion(s32[2048,1024]{1,0:T(8,128)} %param.6), kind=kLoop, calls=%fused_computation.2 | loop fusion | flops 8386560 | bytes 8396800 | tf_op jit(solution)/shard_map/reduce_sum | solution.py:32
  11.7 11.5 %all-reduce.1 = (f32[1024]{0:T(1024)S(1)}, f32[1024]{0:T(1024)S(1)}) all-reduce(f32[1024]{0:T(1024)S(1)} %get-tuple-element.5, f32[1024]{0:T(1024)S(1)} %get-tuple-element.4), channel_id=1, replica_groups=mesh['samp'=4,'snp'=8] {'samp'}, use_global_device_ids=true, to_apply=%region_3.0 | all-reduce | flops 2048 | bytes 16384 | tf_op jit(solution)/shard_map/psum | solution.py:32
  23.3 4.7 %multiply_convert_fusion = bf16[2048,1024]{1,0:T(8,128)(2,1)S(1)} fusion(s32[2048,1024]{1,0:T(8,128)} %param.6, f32[1024]{0:T(1024)S(1)} %get-tuple-element.22, f32[1024]{0:T(1024)S(1)} %get-tuple-element.21), kind=kLoop, calls=%fused_computation | loop fusion | flops 8388608 | bytes 12591104 | tf_op jit(solution)/shard_map/convert_element_type | solution.py:35
  28.3 1.4 collective-permute-start.2
  29.8 1.3 collective-permute-start.3
  31.1 2.3 %collective-permute-done.2 = bf16[2048,512]{1,0:T(8,128)(2,1)S(1)} collective-permute-done((bf16[2048,512]{1,0:T(8,128)(2,1)S(1)}, bf16[2048,512]{1,0:T(8,128)(2,1)S(1)}, u32[]{:S(2)}, u32[]{:S(2)}) %collective-permute-start.2) | collective-permute-done | bytes 2097184 | tf_op jit(solution)/shard_map/ppermute | solution.py:17
  33.4 1.8 fusion.2
  35.2 1.8 fusion.3
  37.5 1.8 fusion.1
  39.3 1.8 fusion
  41.1 2.9 %pad_maximum_fusion.2 = f32[1024,1536]{1,0:T(8,128)} fusion(f32[256,1536]{1,0:T(8,128)S(1)} %fusion, f32[256,1536]{1,0:T(8,128)S(1)} %fusion.1, f32[256,1536]{1,0:T(8,128)S(1)} %fusion.2, f32[256,1536]{1,0:T(8,128)S(1)} %fusion.3), kind=kLoop, calls=%fused_computation.5 | loop fusion | flops 4718592 | bytes 12582912 | tf_op jit(solution)/shard_map/concatenate | solution.py:58
  44.8 23.7 %collective-permute-start = (bf16[2,512]{1,0:T(2,128)(2,1)S(1)}, bf16[2,512]{1,0:T(2,128)(2,1)S(1)}, u32[]{:S(2)}, u32[]{:S(2)}) collective-permute-start(bf16[2,512]{1,0:T(2,128)(2,1)S(1)} %get-tuple-element.18), channel_id=1, source_target_pairs={{0,1},{1,2},{2,3},{3,4},{4,5},{5,6},{6,7},{8,9},{9,10},{10,11},{11... | collective-permute-start | bytes 6152 | tf_op jit(solution)/shard_map/ppermute | solution.py:17
  68.5 1.3 collective-permute-start.1
  71.4 1.4 collective-permute-done.1
  72.9 62.5 %reduce-scatter.2.cloned.1.call-done = f32[256,1536]{1,0:T(8,128)} async-done(((f32[1024,1536]{1,0:T(8,128)}), f32[256,1536]{1,0:T(8,128)}) %reduce-scatter.2.cloned.1.call-update) | async-done | bytes 1572880 | tf_op jit(solution)/shard_map/reduce_scatter | solution.py:57
  135.5 3.0 %fusion.4 = f32[128,256]{1,0:T(8,128)S(1)} fusion(f32[256,1536]{1,0:T(8,128)} %reduce-scatter.2.cloned.1.call-done, s32[1536]{0:T(1024)S(1)} %get-tuple-element.23, s32[1536]{0:T(1024)S(1)} %iota_add_fusion, s32[256]{0:T(256)S(1)} %dynamic_slice.41, s32[256]{0:T(256)S(1)} %dynamic_slice.38, s32[256]{0:T(256)S(1)} %dynamic_slice.37, ...), kind=kOutput, calls=%fused_computation.10 | convolution fusion | flops 608698368 | bytes 1725440 | tf_op jit(solution)/shard_map/dot_general | solution.py:85
  138.5 10.1 %all_gather.3 = f32[128,1024]{1,0:T(8,128)S(1)} all-gather(f32[128,256]{1,0:T(8,128)S(1)} %fusion.4), channel_id=1, replica_groups=mesh['samp'=4,'snp'=8] {'samp'}, dimensions={1}, use_global_device_ids=true | all-gather | bytes 655360 | tf_op jit(solution)/shard_map/all_gather | solution.py:92
  149.9 1.2 fusion.30
  155.6 4.6 %all-to-all-start = ((f32[8,16,1024]{2,1,0:T(8,128)}), f32[8,16,1024]{2,1,0:T(8,128)S(1)}, u32[]{:S(2)}, u32[]{:S(2)}) async-start(f32[8,16,1024]{2,1,0:T(8,128)} %fusion.36), calls=%async_computation.1 | async-start | bytes 1048576 | tf_op jit(solution)/shard_map/all_to_all | solution.py:108
  160.1 1.4 pad_maximum_fusion.10
  161.7 19.6 %all-reduce = (f32[2,128]{1,0:T(2,128)S(1)}, f32[2]{0:T(128)S(1)}) all-reduce(f32[2,128]{1,0:T(2,128)S(1)} %pad_maximum_fusion.9, f32[2]{0:T(128)S(1)} %pad_maximum_fusion.10), channel_id=1, replica_groups=mesh['samp'=4,'snp'=8] {'snp'}, use_global_device_ids=true, to_apply=%region_9.10 | all-reduce | flops 258 | bytes 2064 | tf_op jit(solution)/shard_map/psum | solution.py:104
  182.4 25.6 %all-reduce.4.cloned.1.call-done = f32[128,128]{1,0:T(8,128)} async-done(((f32[128,128]{1,0:T(8,128)}), f32[128,128]{1,0:T(8,128)}) %all-reduce.4.cloned.1.call-update) | async-done | bytes 65552 | tf_op jit(solution)/shard_map/psum | solution.py:104
  208.0 1.5 broadcast_multiply_fusion
  209.5 0.8 copy.11
  (41 shorter events, 10.2 us)
Async XLA Ops:
  7.2 128.3 %reduce-scatter.2.cloned.1.call-start = ((), (), s32[]{:S(2)}) async-start(), calls=%async_computation.2 | async-start | bytes 7864320 | tf_op jit(solution)/shard_map/reduce_scatter | solution.py:57
  28.3 5.1 %collective-permute-start.2 = (bf16[2048,512]{1,0:T(8,128)(2,1)S(1)}, bf16[2048,512]{1,0:T(8,128)(2,1)S(1)}, u32[]{:S(2)}, u32[]{:S(2)}) collective-permute-start(bf16[2048,512]{1,0:T(8,128)(2,1)S(1)} %get-tuple-element.14), channel_id=1, source_target_pairs={{0,1},{1,2},{2,3},{3,4},{4,5},{5,6},{6,7},{8,9},{9,10},{10,11},{11... | collective-permute-start | bytes 6291464 | tf_op jit(solution)/shard_map/ppermute | solution.py:17
  29.8 7.7 %collective-permute-start.3 = (bf16[2048,512]{1,0:T(8,128)(2,1)S(1)}, bf16[2048,512]{1,0:T(8,128)(2,1)S(1)}, u32[]{:S(2)}, u32[]{:S(2)}) collective-permute-start(bf16[2048,512]{1,0:T(8,128)(2,1)S(1)} %get-tuple-element.15), channel_id=1, source_target_pairs={{1,0},{2,1},{3,2},{4,3},{5,4},{6,5},{7,6},{9,8},{10,9},{11,10},{12... | collective-permute-start | bytes 6291464 | tf_op jit(solution)/shard_map/ppermute | solution.py:19
  44.0 0.7 copy-start.2
  44.0 0.7 copy-start.1
  44.1 105.2 %copy-start = (f32[1024]{0:T(1024)S(1)}, f32[1024]{0:T(1024)}, u32[]{:S(2)}) copy-start(f32[1024]{0:T(1024)} %param.11) | copy-start | bytes 12292
  44.1 163.9 %all-reduce.4.cloned.1.call-start = ((), (), s32[]{:S(2)}) async-start(), calls=%async_computation.3 | async-start | bytes 131072 | tf_op jit(solution)/shard_map/psum | solution.py:104
  44.8 26.6 %collective-permute-start = (bf16[2,512]{1,0:T(2,128)(2,1)S(1)}, bf16[2,512]{1,0:T(2,128)(2,1)S(1)}, u32[]{:S(2)}, u32[]{:S(2)}) collective-permute-start(bf16[2,512]{1,0:T(2,128)(2,1)S(1)} %get-tuple-element.18), channel_id=1, source_target_pairs={{0,1},{1,2},{2,3},{3,4},{4,5},{5,6},{6,7},{8,9},{9,10},{10,11},{11... | collective-permute-start | bytes 6152 | tf_op jit(solution)/shard_map/ppermute | solution.py:17
  68.5 4.3 %collective-permute-start.1 = (bf16[2,512]{1,0:T(2,128)(2,1)S(1)}, bf16[2,512]{1,0:T(2,128)(2,1)S(1)}, u32[]{:S(2)}, u32[]{:S(2)}) collective-permute-start(bf16[2,512]{1,0:T(2,128)(2,1)S(1)} %get-tuple-element.19), channel_id=1, source_target_pairs={{1,0},{2,1},{3,2},{4,3},{5,4},{6,5},{7,6},{9,8},{10,9},{11,10},{12... | collective-permute-start | bytes 6152 | tf_op jit(solution)/shard_map/ppermute | solution.py:19
  155.6 53.9 %all-to-all-start = ((f32[8,16,1024]{2,1,0:T(8,128)}), f32[8,16,1024]{2,1,0:T(8,128)S(1)}, u32[]{:S(2)}, u32[]{:S(2)}) async-start(f32[8,16,1024]{2,1,0:T(8,128)} %fusion.36), calls=%async_computation.1 | async-start | bytes 1048576 | tf_op jit(solution)/shard_map/all_to_all | solution.py:108
Sparse Core Ops, SparseCore 0:
  44.2 91.2 reduce-scatter.1
  151.3 56.6 all-reduce.3
